TPU v7x, 32 devices: a 4x4x1 block of a 4x4x8 slice. The times are simulated.
32 devices in a mesh: dp: 1 (over z), tp: 4 (over y), pp: 8 (over x, core).
Axes of the slice: x: 4, y: 4, z: 1, core: 2. Of those that a mesh axis runs over, the one named last changes fastest.
The devices are a block of a 4x4x8 slice.
Arguments:
- hidden_in: bfloat16 [6, 1, 768, 1536], P(None, 'dp')
- positions: int32 [6, 1, 768], P(None, 'dp')
- ln_params: float32 [8, 4, 1536], P('pp')
- w_qkv: bfloat16 [8, 1536, 3, 16, 96], P('pp', None, None, 'tp')
- b_qkv: float32 [8, 3, 16, 96], P('pp', None, 'tp')
- w_out: bfloat16 [8, 16, 96, 1536], P('pp', 'tp')
- w_up: bfloat16 [8, 1536, 6144], P('pp', None, 'tp')
- b_up: float32 [8, 6144], P('pp', 'tp')
- w_down: bfloat16 [8, 6144, 1536], P('pp', 'tp')
- b_res: float32 [8, 2, 1536], P('pp')
Outputs:
- output: bfloat16 [8, 6, 1, 768, 1536], P('pp', None, 'dp')
All inputs are finite; a program needn't handle non-finite values.
Results may differ from a plain program's by a relative error of at most 0.02.
Values are sent between devices in bfloat16 or wider.
A program may use at most 768 MiB of HBM per device.

v0:
```python
import jax
import jax.numpy as jnp
from jax import lax
from jax.sharding import PartitionSpec as P


def layer_norm(hidden, ln_gain, ln_shift):
    hid_f32 = hidden.astype(jnp.float32)
    row_mean = jnp.mean(hid_f32, axis=-1, keepdims=True)
    centred = hid_f32 - row_mean
    row_var = jnp.mean(centred * centred, axis=-1, keepdims=True)
    return (centred * lax.rsqrt(row_var + 1e-5) * ln_gain + ln_shift).astype(jnp.bfloat16)


def attend(qkv_h, pos_rows, head_first, head_total):
    query_h = qkv_h[:, :, 0]
    key_h = qkv_h[:, :, 1]
    value_h = qkv_h[:, :, 2]
    seq_len = qkv_h.shape[1]
    n_local = qkv_h.shape[3]
    score_scale = qkv_h.shape[4] ** -0.5
    scores = jnp.einsum("bqhe,bkhe->bhqk", query_h, key_h, preferred_element_type=jnp.float32) * score_scale
    head_ids = (head_first + jnp.arange(n_local)).astype(jnp.float32)
    slopes = jnp.exp2(-8.0 * (head_ids + 1.0) / head_total)
    rel_pos = (pos_rows[:, :, None] - pos_rows[:, None, :]).astype(jnp.float32)
    scores = scores - slopes[None, :, None, None] * rel_pos[:, None, :, :]
    causal = lax.broadcasted_iota(jnp.int32, (seq_len, seq_len), 0) >= lax.broadcasted_iota(jnp.int32, (seq_len, seq_len), 1)
    scores = jnp.where(causal, scores, -1e30)
    probs_bf = jax.nn.softmax(scores, axis=-1).astype(jnp.bfloat16)
    return jnp.einsum("bhqk,bkhe->bqhe", probs_bf, value_h, preferred_element_type=jnp.float32).astype(jnp.bfloat16)


def stage_layer(hidden, pos_rows, weights, head_first, head_total):
    ln_p, w_qkv, b_qkv, w_out, w_up, b_up, w_down, b_res = weights
    normed = layer_norm(hidden, ln_p[0], ln_p[1])
    qkv_f = jnp.einsum("bsd,dche->bsche", normed, w_qkv, preferred_element_type=jnp.float32) + b_qkv
    context = attend(qkv_f.astype(jnp.bfloat16), pos_rows, head_first, head_total)
    attn_part = jnp.einsum("bshe,hed->bsd", context, w_out, preferred_element_type=jnp.float32).astype(jnp.bfloat16)
    attn_sum = lax.psum(attn_part, "tp")
    resid_mid = (hidden.astype(jnp.float32) + attn_sum.astype(jnp.float32) + b_res[0]).astype(jnp.bfloat16)
    normed_mlp = layer_norm(resid_mid, ln_p[2], ln_p[3])
    up_f = jnp.einsum("bsd,df->bsf", normed_mlp, w_up, preferred_element_type=jnp.float32) + b_up
    gelu_out = jax.nn.gelu(up_f, approximate=True).astype(jnp.bfloat16)
    mlp_part = jnp.einsum("bsf,fd->bsd", gelu_out, w_down, preferred_element_type=jnp.float32).astype(jnp.bfloat16)
    mlp_sum = lax.psum(mlp_part, "tp")
    return (resid_mid.astype(jnp.float32) + mlp_sum.astype(jnp.float32) + b_res[1]).astype(jnp.bfloat16)


def solution(mesh):
    tp_size = mesh.shape["tp"]
    pp_size = mesh.shape["pp"]
    shift_perm = [(src_id, src_id + 1) for src_id in range(pp_size - 1)]

    def stage_body(hidden_in, positions, ln_params, w_qkv, b_qkv, w_out, w_up, b_up, w_down, b_res):
        stage_id = lax.axis_index("pp")
        n_local = w_qkv.shape[3]
        head_first = lax.axis_index("tp") * n_local
        head_total = n_local * tp_size
        weights = (ln_params[0], w_qkv[0], b_qkv[0], w_out[0], w_up[0], b_up[0], w_down[0], b_res[0])
        n_micro = hidden_in.shape[0]

        def tick_step(tick_id, loop_carry):
            received, stage_acts = loop_carry
            micro_id = tick_id - stage_id
            is_valid = (micro_id >= 0) & (micro_id < n_micro)
            micro_idx = jnp.clip(micro_id, 0, n_micro - 1)
            fresh_in = lax.dynamic_index_in_dim(hidden_in, micro_idx, 0, keepdims=False)
            hidden = jnp.where(stage_id == 0, fresh_in, received)
            pos_rows = lax.dynamic_index_in_dim(positions, micro_idx, 0, keepdims=False)
            result = stage_layer(hidden, pos_rows, weights, head_first, head_total)
            previous = lax.dynamic_index_in_dim(stage_acts, micro_idx, 0, keepdims=False)
            stage_acts = lax.dynamic_update_index_in_dim(stage_acts, jnp.where(is_valid, result, previous), micro_idx, 0)
            sent_out = lax.ppermute(result, "pp", perm=shift_perm)
            return sent_out, stage_acts

        init_carry = (jnp.zeros(hidden_in.shape[1:], jnp.bfloat16), jnp.zeros(hidden_in.shape, jnp.bfloat16))
        _, stage_acts = lax.fori_loop(0, n_micro + pp_size - 1, tick_step, init_carry)
        return stage_acts[None]

    in_specs = (P(None, "dp", None, None), P(None, "dp", None), P("pp", None, None), P("pp", None, None, "tp", None), P("pp", None, "tp", None), P("pp", "tp", None, None), P("pp", None, "tp"), P("pp", "tp"), P("pp", "tp", None), P("pp", None, None))
    return jax.shard_map(stage_body, mesh=mesh, in_specs=in_specs, out_specs=P("pp", None, "dp", None, None), check_vma=False)
```

profile of v0, /device:TPU:103, one launch (start us, length us, event | category | flops | bytes accessed | tf_op | source)
XLA Modules:
  0.0 2594.5 jit_solution(1051552377650024187)
XLA Ops:
  14.6 2573.3 %while.17 = (s32[]{:T(128)}, bf16[1,768,1536]{2,1,0:T(8,128)(2,1)}, bf16[6,1,768,1536]{3,2,1,0:T(8,128)(2,1)}, pred[]{:T(512)}, s32[]{:T(128)}, /*index=5*/bf16[...) while((s32[]{:T(128)}, bf16[1,768,1536]{2,1,0:T(8,128)(2,1)}, ...), condition=%wide.region_9.10_spmd, body=%wide.region_0.9_spmd.sunk | while | flops 11859298304 | bytes 174811152 | solution.py:77
  43.7 60.1 %all-reduce.3.cloned.1.call-done = bf16[1,768,1536]{2,1,0:T(8,128)(2,1)} async-done(((bf16[1,768,1536]{2,1,0:T(8,128)(2,1)}), bf16[1,768,1536]{2,1,0:T(8,128)(2,1)}) %all-reduce.3.cloned.1.call-update) | async-done | bytes 2359312 | tf_op jit(solution)/shard_map/while/body/eval_jaxpr/psum | solution.py:39
  125.5 54.2 %all-reduce.5.cloned.1.call-done = bf16[1,768,1536]{2,1,0:T(8,128)(2,1)} async-done(((bf16[1,768,1536]{2,1,0:T(8,128)(2,1)}), bf16[1,768,1536]{2,1,0:T(8,128)(2,1)}) %all-reduce.5.cloned.1.call-update) | async-done | bytes 2359312 | tf_op jit(solution)/shard_map/while/body/eval_jaxpr/psum | solution.py:45
  222.5 80.8 %all-reduce.3.cloned.1.call-done = bf16[1,768,1536]{2,1,0:T(8,128)(2,1)} async-done(((bf16[1,768,1536]{2,1,0:T(8,128)(2,1)}), bf16[1,768,1536]{2,1,0:T(8,128)(2,1)}) %all-reduce.3.cloned.1.call-update) | async-done | bytes 2359312 | tf_op jit(solution)/shard_map/while/body/eval_jaxpr/psum | solution.py:39
  325.0 54.2 %all-reduce.5.cloned.1.call-done = bf16[1,768,1536]{2,1,0:T(8,128)(2,1)} async-done(((bf16[1,768,1536]{2,1,0:T(8,128)(2,1)}), bf16[1,768,1536]{2,1,0:T(8,128)(2,1)}) %all-reduce.5.cloned.1.call-update) | async-done | bytes 2359312 | tf_op jit(solution)/shard_map/while/body/eval_jaxpr/psum | solution.py:45
  422.0 80.8 %all-reduce.3.cloned.1.call-done = bf16[1,768,1536]{2,1,0:T(8,128)(2,1)} async-done(((bf16[1,768,1536]{2,1,0:T(8,128)(2,1)}), bf16[1,768,1536]{2,1,0:T(8,128)(2,1)}) %all-reduce.3.cloned.1.call-update) | async-done | bytes 2359312 | tf_op jit(solution)/shard_map/while/body/eval_jaxpr/psum | solution.py:39
  524.5 54.2 %all-reduce.5.cloned.1.call-done = bf16[1,768,1536]{2,1,0:T(8,128)(2,1)} async-done(((bf16[1,768,1536]{2,1,0:T(8,128)(2,1)}), bf16[1,768,1536]{2,1,0:T(8,128)(2,1)}) %all-reduce.5.cloned.1.call-update) | async-done | bytes 2359312 | tf_op jit(solution)/shard_map/while/body/eval_jaxpr/psum | solution.py:45
  621.6 80.8 %all-reduce.3.cloned.1.call-done = bf16[1,768,1536]{2,1,0:T(8,128)(2,1)} async-done(((bf16[1,768,1536]{2,1,0:T(8,128)(2,1)}), bf16[1,768,1536]{2,1,0:T(8,128)(2,1)}) %all-reduce.3.cloned.1.call-update) | async-done | bytes 2359312 | tf_op jit(solution)/shard_map/while/body/eval_jaxpr/psum | solution.py:39
  724.1 54.2 %all-reduce.5.cloned.1.call-done = bf16[1,768,1536]{2,1,0:T(8,128)(2,1)} async-done(((bf16[1,768,1536]{2,1,0:T(8,128)(2,1)}), bf16[1,768,1536]{2,1,0:T(8,128)(2,1)}) %all-reduce.5.cloned.1.call-update) | async-done | bytes 2359312 | tf_op jit(solution)/shard_map/while/body/eval_jaxpr/psum | solution.py:45
  821.1 80.8 %all-reduce.3.cloned.1.call-done = bf16[1,768,1536]{2,1,0:T(8,128)(2,1)} async-done(((bf16[1,768,1536]{2,1,0:T(8,128)(2,1)}), bf16[1,768,1536]{2,1,0:T(8,128)(2,1)}) %all-reduce.3.cloned.1.call-update) | async-done | bytes 2359312 | tf_op jit(solution)/shard_map/while/body/eval_jaxpr/psum | solution.py:39
  923.6 54.2 %all-reduce.5.cloned.1.call-done = bf16[1,768,1536]{2,1,0:T(8,128)(2,1)} async-done(((bf16[1,768,1536]{2,1,0:T(8,128)(2,1)}), bf16[1,768,1536]{2,1,0:T(8,128)(2,1)}) %all-reduce.5.cloned.1.call-update) | async-done | bytes 2359312 | tf_op jit(solution)/shard_map/while/body/eval_jaxpr/psum | solution.py:45
  1020.6 80.8 %all-reduce.3.cloned.1.call-done = bf16[1,768,1536]{2,1,0:T(8,128)(2,1)} async-done(((bf16[1,768,1536]{2,1,0:T(8,128)(2,1)}), bf16[1,768,1536]{2,1,0:T(8,128)(2,1)}) %all-reduce.3.cloned.1.call-update) | async-done | bytes 2359312 | tf_op jit(solution)/shard_map/while/body/eval_jaxpr/psum | solution.py:39
  1123.1 54.2 %all-reduce.5.cloned.1.call-done = bf16[1,768,1536]{2,1,0:T(8,128)(2,1)} async-done(((bf16[1,768,1536]{2,1,0:T(8,128)(2,1)}), bf16[1,768,1536]{2,1,0:T(8,128)(2,1)}) %all-reduce.5.cloned.1.call-update) | async-done | bytes 2359312 | tf_op jit(solution)/shard_map/while/body/eval_jaxpr/psum | solution.py:45
  1220.1 80.8 %all-reduce.3.cloned.1.call-done = bf16[1,768,1536]{2,1,0:T(8,128)(2,1)} async-done(((bf16[1,768,1536]{2,1,0:T(8,128)(2,1)}), bf16[1,768,1536]{2,1,0:T(8,128)(2,1)}) %all-reduce.3.cloned.1.call-update) | async-done | bytes 2359312 | tf_op jit(solution)/shard_map/while/body/eval_jaxpr/psum | solution.py:39
  1322.7 54.2 %all-reduce.5.cloned.1.call-done = bf16[1,768,1536]{2,1,0:T(8,128)(2,1)} async-done(((bf16[1,768,1536]{2,1,0:T(8,128)(2,1)}), bf16[1,768,1536]{2,1,0:T(8,128)(2,1)}) %all-reduce.5.cloned.1.call-update) | async-done | bytes 2359312 | tf_op jit(solution)/shard_map/while/body/eval_jaxpr/psum | solution.py:45
  1419.7 80.8 %all-reduce.3.cloned.1.call-done = bf16[1,768,1536]{2,1,0:T(8,128)(2,1)} async-done(((bf16[1,768,1536]{2,1,0:T(8,128)(2,1)}), bf16[1,768,1536]{2,1,0:T(8,128)(2,1)}) %all-reduce.3.cloned.1.call-update) | async-done | bytes 2359312 | tf_op jit(solution)/shard_map/while/body/eval_jaxpr/psum | solution.py:39
  1619.2 80.8 %all-reduce.3.cloned.1.call-done = bf16[1,768,1536]{2,1,0:T(8,128)(2,1)} async-done(((bf16[1,768,1536]{2,1,0:T(8,128)(2,1)}), bf16[1,768,1536]{2,1,0:T(8,128)(2,1)}) %all-reduce.3.cloned.1.call-update) | async-done | bytes 2359312 | tf_op jit(solution)/shard_map/while/body/eval_jaxpr/psum | solution.py:39
  1721.7 54.2 %all-reduce.5.cloned.1.call-done = bf16[1,768,1536]{2,1,0:T(8,128)(2,1)} async-done(((bf16[1,768,1536]{2,1,0:T(8,128)(2,1)}), bf16[1,768,1536]{2,1,0:T(8,128)(2,1)}) %all-reduce.5.cloned.1.call-update) | async-done | bytes 2359312 | tf_op jit(solution)/shard_map/while/body/eval_jaxpr/psum | solution.py:45
  1818.8 80.8 %all-reduce.3.cloned.1.call-done = bf16[1,768,1536]{2,1,0:T(8,128)(2,1)} async-done(((bf16[1,768,1536]{2,1,0:T(8,128)(2,1)}), bf16[1,768,1536]{2,1,0:T(8,128)(2,1)}) %all-reduce.3.cloned.1.call-update) | async-done | bytes 2359312 | tf_op jit(solution)/shard_map/while/body/eval_jaxpr/psum | solution.py:39
  2018.3 80.8 %all-reduce.3.cloned.1.call-done = bf16[1,768,1536]{2,1,0:T(8,128)(2,1)} async-done(((bf16[1,768,1536]{2,1,0:T(8,128)(2,1)}), bf16[1,768,1536]{2,1,0:T(8,128)(2,1)}) %all-reduce.3.cloned.1.call-update) | async-done | bytes 2359312 | tf_op jit(solution)/shard_map/while/body/eval_jaxpr/psum | solution.py:39
  2120.8 54.2 %all-reduce.5.cloned.1.call-done = bf16[1,768,1536]{2,1,0:T(8,128)(2,1)} async-done(((bf16[1,768,1536]{2,1,0:T(8,128)(2,1)}), bf16[1,768,1536]{2,1,0:T(8,128)(2,1)}) %all-reduce.5.cloned.1.call-update) | async-done | bytes 2359312 | tf_op jit(solution)/shard_map/while/body/eval_jaxpr/psum | solution.py:45
  2217.8 80.8 %all-reduce.3.cloned.1.call-done = bf16[1,768,1536]{2,1,0:T(8,128)(2,1)} async-done(((bf16[1,768,1536]{2,1,0:T(8,128)(2,1)}), bf16[1,768,1536]{2,1,0:T(8,128)(2,1)}) %all-reduce.3.cloned.1.call-update) | async-done | bytes 2359312 | tf_op jit(solution)/shard_map/while/body/eval_jaxpr/psum | solution.py:39
  2417.3 80.8 %all-reduce.3.cloned.1.call-done = bf16[1,768,1536]{2,1,0:T(8,128)(2,1)} async-done(((bf16[1,768,1536]{2,1,0:T(8,128)(2,1)}), bf16[1,768,1536]{2,1,0:T(8,128)(2,1)}) %all-reduce.3.cloned.1.call-update) | async-done | bytes 2359312 | tf_op jit(solution)/shard_map/while/body/eval_jaxpr/psum | solution.py:39
  2519.8 54.2 %all-reduce.5.cloned.1.call-done = bf16[1,768,1536]{2,1,0:T(8,128)(2,1)} async-done(((bf16[1,768,1536]{2,1,0:T(8,128)(2,1)}), bf16[1,768,1536]{2,1,0:T(8,128)(2,1)}) %all-reduce.5.cloned.1.call-update) | async-done | bytes 2359312 | tf_op jit(solution)/shard_map/while/body/eval_jaxpr/psum | solution.py:45
  (481 shorter events, 1008.3 us)
Async XLA Ops:
  43.5 136.2 %all-reduce.5.cloned.1.call-start = ((), (), s32[]{:S(2)}) async-start(), calls=%async_computation.1 | async-start | bytes 4718592 | tf_op jit(solution)/shard_map/while/body/eval_jaxpr/psum | solution.py:45
  193.6 109.7 %all-reduce.3.cloned.1.call-start = ((), (), s32[]{:S(2)}) async-start(), calls=%async_computation | async-start | bytes 4718592 | tf_op jit(solution)/shard_map/while/body/eval_jaxpr/psum | solution.py:39
  222.4 156.8 %all-reduce.5.cloned.1.call-start = ((), (), s32[]{:S(2)}) async-start(), calls=%async_computation.1 | async-start | bytes 4718592 | tf_op jit(solution)/shard_map/while/body/eval_jaxpr/psum | solution.py:45
  421.9 156.8 %all-reduce.5.cloned.1.call-start = ((), (), s32[]{:S(2)}) async-start(), calls=%async_computation.1 | async-start | bytes 4718592 | tf_op jit(solution)/shard_map/while/body/eval_jaxpr/psum | solution.py:45
  592.6 109.7 %all-reduce.3.cloned.1.call-start = ((), (), s32[]{:S(2)}) async-start(), calls=%async_computation | async-start | bytes 4718592 | tf_op jit(solution)/shard_map/while/body/eval_jaxpr/psum | solution.py:39
  621.4 156.8 %all-reduce.5.cloned.1.call-start = ((), (), s32[]{:S(2)}) async-start(), calls=%async_computation.1 | async-start | bytes 4718592 | tf_op jit(solution)/shard_map/while/body/eval_jaxpr/psum | solution.py:45
  792.2 109.7 %all-reduce.3.cloned.1.call-start = ((), (), s32[]{:S(2)}) async-start(), calls=%async_computation | async-start | bytes 4718592 | tf_op jit(solution)/shard_map/while/body/eval_jaxpr/psum | solution.py:39
  820.9 156.8 %all-reduce.5.cloned.1.call-start = ((), (), s32[]{:S(2)}) async-start(), calls=%async_computation.1 | async-start | bytes 4718592 | tf_op jit(solution)/shard_map/while/body/eval_jaxpr/psum | solution.py:45
  991.7 109.7 %all-reduce.3.cloned.1.call-start = ((), (), s32[]{:S(2)}) async-start(), calls=%async_computation | async-start | bytes 4718592 | tf_op jit(solution)/shard_map/while/body/eval_jaxpr/psum | solution.py:39
  1020.5 156.8 %all-reduce.5.cloned.1.call-start = ((), (), s32[]{:S(2)}) async-start(), calls=%async_computation.1 | async-start | bytes 4718592 | tf_op jit(solution)/shard_map/while/body/eval_jaxpr/psum | solution.py:45
  1191.2 109.7 %all-reduce.3.cloned.1.call-start = ((), (), s32[]{:S(2)}) async-start(), calls=%async_computation | async-start | bytes 4718592 | tf_op jit(solution)/shard_map/while/body/eval_jaxpr/psum | solution.py:39
  1220.0 156.8 %all-reduce.5.cloned.1.call-start = ((), (), s32[]{:S(2)}) async-start(), calls=%async_computation.1 | async-start | bytes 4718592 | tf_op jit(solution)/shard_map/while/body/eval_jaxpr/psum | solution.py:45
  1390.8 109.7 %all-reduce.3.cloned.1.call-start = ((), (), s32[]{:S(2)}) async-start(), calls=%async_computation | async-start | bytes 4718592 | tf_op jit(solution)/shard_map/while/body/eval_jaxpr/psum | solution.py:39
  1419.6 156.8 %all-reduce.5.cloned.1.call-start = ((), (), s32[]{:S(2)}) async-start(), calls=%async_computation.1 | async-start | bytes 4718592 | tf_op jit(solution)/shard_map/while/body/eval_jaxpr/psum | solution.py:45
  1590.3 109.7 %all-reduce.3.cloned.1.call-start = ((), (), s32[]{:S(2)}) async-start(), calls=%async_computation | async-start | bytes 4718592 | tf_op jit(solution)/shard_map/while/body/eval_jaxpr/psum | solution.py:39
  1619.1 156.8 %all-reduce.5.cloned.1.call-start = ((), (), s32[]{:S(2)}) async-start(), calls=%async_computation.1 | async-start | bytes 4718592 | tf_op jit(solution)/shard_map/while/body/eval_jaxpr/psum | solution.py:45
  1789.8 109.7 %all-reduce.3.cloned.1.call-start = ((), (), s32[]{:S(2)}) async-start(), calls=%async_computation | async-start | bytes 4718592 | tf_op jit(solution)/shard_map/while/body/eval_jaxpr/psum | solution.py:39
  1818.6 156.8 %all-reduce.5.cloned.1.call-start = ((), (), s32[]{:S(2)}) async-start(), calls=%async_computation.1 | async-start | bytes 4718592 | tf_op jit(solution)/shard_map/while/body/eval_jaxpr/psum | solution.py:45
  1989.3 109.7 %all-reduce.3.cloned.1.call-start = ((), (), s32[]{:S(2)}) async-start(), calls=%async_computation | async-start | bytes 4718592 | tf_op jit(solution)/shard_map/while/body/eval_jaxpr/psum | solution.py:39
  2018.1 156.8 %all-reduce.5.cloned.1.call-start = ((), (), s32[]{:S(2)}) async-start(), calls=%async_computation.1 | async-start | bytes 4718592 | tf_op jit(solution)/shard_map/while/body/eval_jaxpr/psum | solution.py:45
  2188.9 109.7 %all-reduce.3.cloned.1.call-start = ((), (), s32[]{:S(2)}) async-start(), calls=%async_computation | async-start | bytes 4718592 | tf_op jit(solution)/shard_map/while/body/eval_jaxpr/psum | solution.py:39
  2217.7 156.8 %all-reduce.5.cloned.1.call-start = ((), (), s32[]{:S(2)}) async-start(), calls=%async_computation.1 | async-start | bytes 4718592 | tf_op jit(solution)/shard_map/while/body/eval_jaxpr/psum | solution.py:45
  2388.4 109.7 %all-reduce.3.cloned.1.call-start = ((), (), s32[]{:S(2)}) async-start(), calls=%async_computation | async-start | bytes 4718592 | tf_op jit(solution)/shard_map/while/body/eval_jaxpr/psum | solution.py:39
  2417.2 156.8 %all-reduce.5.cloned.1.call-start = ((), (), s32[]{:S(2)}) async-start(), calls=%async_computation.1 | async-start | bytes 4718592 | tf_op jit(solution)/shard_map/while/body/eval_jaxpr/psum | solution.py:45
  (71 other events, 1153.3 us)
Sparse Core Ops, SparseCore 0:
  43.6 60.0 all-reduce.2
  122.2 57.4 all-reduce.4
  222.5 80.7 all-reduce.2
  321.7 57.4 all-reduce.4
  422.0 80.7 all-reduce.2
  521.2 57.4 all-reduce.4
  621.6 80.7 all-reduce.2
  720.8 57.4 all-reduce.4
  821.1 80.7 all-reduce.2
  920.3 57.4 all-reduce.4
  1020.6 80.7 all-reduce.2
  1119.8 57.4 all-reduce.4
  1220.1 80.7 all-reduce.2
  1319.3 57.4 all-reduce.4
  1419.7 80.7 all-reduce.2
  1619.2 80.7 all-reduce.2
  1718.4 57.4 all-reduce.4
  1818.7 80.7 all-reduce.2
  2018.2 80.7 all-reduce.2
  2117.5 57.4 all-reduce.4
  2217.8 80.7 all-reduce.2
  2317.0 57.4 all-reduce.4
  2417.3 80.7 all-reduce.2
  2516.5 57.4 all-reduce.4
  (2 shorter events, 114.8 us)
where the time goes:
time: 2620 us; the launch traced here: 2590 us
  waiting for transfers between devices  1810 us (69%)
  matrix products  442 us (17%)
  other arithmetic  213 us (8%)
  local copies, waits for them, and re-layouts  99.2 us (4%)
    psum x13, waiting for transfers between devices, stage_layer(): attn_sum = lax.psum(attn_part, 'tp')  1030 us
    psum x13, waiting for transfers between devices, stage_layer(): mlp_sum = lax.psum(mlp_part, 'tp')  704 us
    dot_general x13, matrix products, stage_layer(): jnp.einsum('bsf,fd->bsd', gelu_out, w_down, preferred_element_type=jnp.fl...  176 us
    sub x13, matrix products, attend(): probs_bf = jax.nn.softmax(scores, axis=-1).astype(jnp.bfloat16)  126 us
    dot_general x13, matrix products, stage_layer(): jnp.einsum('bshe,hed->bsd', context, w_out, preferred_element_type=jnp.fl...  99.6 us
    reduce_sum x26, other arithmetic, layer_norm(): row_mean = jnp.mean(hid_f32, axis=-1, keepdims=True)  76.2 us
    dynamic_update_slice x13, other arithmetic, tick_step(): lax.dynamic_update_index_in_dim(stage_acts, jnp.where(is_valid, result, p...  73.1 us
    ppermute x13, waiting for transfers between devices, tick_step(): sent_out = lax.ppermute(result, 'pp', perm=shift_perm)  72.4 us
  transfers between devices with their start and end apart: 39, of which 39 were waited for; matrix products, arithmetic and copies ran while one was open for 2% of the time, Pallas kernels for 0%

commit v1 on v0

v1 whole, which is shorter than its diff:
```python
import functools

import jax
import jax.numpy as jnp
from jax import lax
from jax.experimental import pallas as pl
from jax.experimental.pallas import tpu as pltpu
from jax.sharding import PartitionSpec as P

MESH = pl.DeviceIdType.MESH
F32 = jnp.float32
BF16 = jnp.bfloat16
CHUNKS = 2
SUBS = 2
LN_ROWS = 32
ATT_ROWS = 96
COLS = 512


class RingGather:
    def __init__(self, view, me, left, right, send, recv, base=0):
        self.view, self.me, self.left, self.right = view, me, left, right
        self.send, self.recv, self.base = send, recv, base

    def _copy(self, owner, half, slot, to):
        ref = self.view(owner, half)
        return pltpu.make_async_remote_copy(
            src_ref=ref, dst_ref=ref, send_sem=self.send.at[self.base + slot], recv_sem=self.recv.at[self.base + slot],
            device_id={"tp": to}, device_id_type=MESH)

    def start(self):
        self._copy(self.me, 0, 0, self.right).start()
        self._copy(self.me, 1, 3, self.left).start()
        self._copy(self.me, 1, 1, self.right).start()
        self._copy(self.me, 0, 4, self.left).start()

    def forward(self):
        self._copy(self.left, 0, 0, self.right).wait_recv()
        self._copy(self.left, 0, 2, self.right).start()
        self._copy(self.right, 1, 3, self.left).wait_recv()
        self._copy(self.right, 1, 5, self.left).start()

    def wait_near(self):
        self._copy(self.left, 1, 1, self.right).wait_recv()
        self._copy(self.right, 0, 4, self.left).wait_recv()

    def wait_far(self):
        far = lax.rem(self.me + 2, 4)
        self._copy(far, 0, 2, self.right).wait_recv()
        self._copy(far, 1, 5, self.left).wait_recv()

    def wait_send(self):
        for slot, owner, half, to in ((0, self.me, 0, self.right), (1, self.me, 1, self.right), (2, self.left, 0, self.right),
                                      (3, self.me, 1, self.left), (4, self.me, 0, self.left), (5, self.right, 1, self.left)):
            self._copy(owner, half, slot, to).wait_send()


def norm_rows(x, gain, shift):
    mean = jnp.mean(x, axis=-1, keepdims=True)
    cent = x - mean
    var = jnp.mean(cent * cent, axis=-1, keepdims=True)
    return (cent * lax.rsqrt(var + 1e-5) * gain + shift).astype(BF16)


def split_quarter(sub, sub_rows):
    quarter = sub_rows // 4
    big = -(-quarter // 32) * 16
    first = big if sub % 2 == 0 else quarter - big
    return (0, first), (first, quarter - first)


def pipeline_kernel(dims, slopes, hidden, pos_col, pos_row, ln_p, w_qkv, b_qkv, w_out, w_up, b_up, w_down, b_res, acts,
                    wq, wo, wu, wd, hin, a, q, kc, vc, ctx, xmid, u, part, r1, r2, msg, hout,
                    wsem, asend, arecv, rsend, rrecv, bsend, brecv, wsend, wrecv, psend, precv, osem, credit):
    n_micro, seq, width, n_local, head_dim, chunks, stages = dims
    size = seq // chunks
    sub_rows = size // SUBS
    quarter = sub_rows // 4
    local = n_local * head_dim
    units = n_micro * chunks
    ff = wu.shape[1]
    me = lax.axis_index("tp")
    stage = lax.axis_index("pp")
    left, right, far = lax.rem(me + 3, 4), lax.rem(me + 1, 4), lax.rem(me + 2, 4)
    before, after = lax.rem(stage + stages - 1, stages), lax.rem(stage + 1, stages)
    first, last = stage == 0, stage == stages - 1
    inner = jnp.logical_not(last)
    subs = range(SUBS)

    def wo_rows(owner, part_id):
        return wo.at[pl.ds(pl.multiple_of(owner * local + part_id * (local // 2), 64), local // 2)]

    own_wo = wo.at[pl.ds(pl.multiple_of(me * local, 128), local)]
    loads = [pltpu.make_async_copy(w_out, own_wo, wsem.at[0]), pltpu.make_async_copy(w_qkv, wq, wsem.at[1]),
             pltpu.make_async_copy(w_up, wu, wsem.at[2]), pltpu.make_async_copy(w_down, wd, wsem.at[3])]
    for load in loads:
        load.start()

    def fetch(unit, slot):
        m, c = unit // chunks, unit % chunks
        return pltpu.make_async_copy(hidden.at[m, pl.ds(pl.multiple_of(c * size, 64), size)], hin.at[slot], precv.at[slot])

    @pl.when(first)
    def _():
        fetch(0, 0).start()

    barrier = pltpu.get_barrier_semaphore()
    for peer in (left, right):
        pl.semaphore_signal(barrier, inc=1, device_id={"tp": peer}, device_id_type=MESH)
    for peer in (before, after):
        pl.semaphore_signal(barrier, inc=1, device_id={"pp": peer}, device_id_type=MESH)
    kc[...] = jnp.zeros_like(kc)
    vc[...] = jnp.zeros_like(vc)
    pl.semaphore_wait(barrier, 4)

    loads[0].wait()
    gather_wo = RingGather(wo_rows, me, left, right, wsend, wrecv)
    gather_wo.start()
    for load in loads[1:]:
        load.wait()

    def finish_wo():
        gather_wo.wait_near()
        gather_wo.wait_far()
        gather_wo.wait_send()

    @pl.when(jnp.logical_not(first))
    def _():
        gather_wo.forward()
        finish_wo()

    def part_rows(s, owner, k):
        offset, rows = split_quarter(s, sub_rows)[k]
        return pl.ds(pl.multiple_of(s * sub_rows + owner * quarter + offset, 16), rows)

    def quarter_rows(s, owner):
        return pl.ds(pl.multiple_of(s * sub_rows + owner * quarter, 16), quarter)

    def ctx_view(s):
        def view(owner, k):
            half = sub_rows // 2
            return ctx.at[pl.ds(s * sub_rows + k * half, half), pl.ds(pl.multiple_of(owner * local, 128), local)]
        return view

    def out_view(s):
        return lambda owner, k: hout.at[part_rows(s, owner, k)]

    gather_ctx = [RingGather(ctx_view(s), me, left, right, asend, arecv, 6 * s) for s in subs]
    gather_out = [RingGather(out_view(s), me, left, right, bsend, brecv, 6 * s) for s in subs]

    def reduce_copy(s, slot, src, dst, to):
        return pltpu.make_async_remote_copy(src_ref=src, dst_ref=dst, send_sem=rsend.at[6 * s + slot], recv_sem=rrecv.at[6 * s + slot],
                                            device_id={"tp": to}, device_id_type=MESH)

    def piece(ref, s, k):
        return ref.at[pl.ds(0, split_quarter(s, sub_rows)[k][1])]

    def copies_first(s):
        return [reduce_copy(s, 0, part.at[part_rows(s, far, 0)], piece(r1.at[s, 0], s, 0), right),
                reduce_copy(s, 1, part.at[part_rows(s, far, 1)], piece(r1.at[s, 1], s, 1), left),
                reduce_copy(s, 2, part.at[part_rows(s, right, 1)], piece(r2.at[s, 0, 1], s, 1), right),
                reduce_copy(s, 3, part.at[part_rows(s, left, 0)], piece(r2.at[s, 1, 0], s, 0), left)]

    def copies_second(s):
        return [reduce_copy(s, 4, piece(msg.at[s, 0], s, 0), piece(r2.at[s, 0, 0], s, 0), right),
                reduce_copy(s, 5, piece(msg.at[s, 1], s, 1), piece(r2.at[s, 1, 1], s, 1), left)]

    def hand_on(s, k, owner, slot):
        rows = quarter_rows(s, owner)
        return pltpu.make_async_remote_copy(src_ref=hout.at[rows], dst_ref=hin.at[slot, rows], send_sem=psend.at[4 * s + k], recv_sem=precv.at[slot],
                                            device_id={"pp": after}, device_id_type=MESH)

    def reduce_middle(s):
        firsts, seconds = copies_first(s), copies_second(s)
        for k, owner in ((0, right), (1, left)):
            rows = split_quarter(s, sub_rows)[k][1]
            firsts[k].wait_recv()
            msg[s, k, :rows, :] = (part[part_rows(s, owner, k), :].astype(F32) + r1[s, k, :rows, :].astype(F32)).astype(BF16)
            seconds[k].start()

    def reduce_end(s, unit):
        for copy in copies_first(s)[2:] + copies_second(s):
            copy.wait_recv()
        for k in range(2):
            n, rows = split_quarter(s, sub_rows)[k][1], part_rows(s, me, k)
            y = part[rows, :].astype(F32) + r2[s, 0, k, :n, :].astype(F32) + r2[s, 1, k, :n, :].astype(F32)
            hout[rows, :] = (xmid[rows, :].astype(F32) + y + b_res[1:2, :]).astype(BF16)
        gather_out[s].start()
        if s == 0:
            @pl.when(inner & (unit > 1))
            def _():
                pl.semaphore_wait(credit, 1)

        @pl.when(inner)
        def _():
            hand_on(s, 0, me, lax.rem(unit, 2)).start()
        for copy in copies_first(s) + copies_second(s):
            copy.wait_send()

    def out_near(s, unit):
        gather_out[s].wait_near()

        @pl.when(inner)
        def _():
            hand_on(s, 1, left, lax.rem(unit, 2)).start()
            hand_on(s, 2, right, lax.rem(unit, 2)).start()

    def out_far(s, unit):
        gather_out[s].wait_far()

        @pl.when(inner)
        def _():
            hand_on(s, 3, far, lax.rem(unit, 2)).start()

    def store_out(unit):
        m, c = unit // chunks, unit % chunks
        return pltpu.make_async_copy(hout, acts.at[m, pl.ds(pl.multiple_of(c * size, 64), size)], osem.at[0])

    def tail_one(unit):
        reduce_middle(SUBS - 1)
        for s in range(SUBS - 1):
            gather_out[s].forward()
            out_near(s, unit)
        reduce_end(SUBS - 1, unit)

    def tail_two(unit):
        gather_out[SUBS - 1].forward()
        for s in range(SUBS - 1):
            out_far(s, unit)

    def tail_three(unit):
        out_near(SUBS - 1, unit)
        out_far(SUBS - 1, unit)
        store_out(unit).start()

    def finish_out(unit):
        for s in subs:
            gather_out[s].wait_send()
        store_out(unit).wait()

        @pl.when(inner)
        def _():
            for s in subs:
                for k, owner in enumerate((me, left, right, far)):
                    hand_on(s, k, owner, lax.rem(unit, 2)).wait_send()

    def norm_into(src, start, count, gain, shift):
        @pl.loop(0, count // LN_ROWS)
        def _(i):
            rows = pl.ds(pl.multiple_of(start + i * LN_ROWS, LN_ROWS), LN_ROWS)
            a[rows, :] = norm_rows(src[rows, :].astype(F32), gain, shift)

    def attention(m, c_static, s):
        base = c_static * size + s * sub_rows
        reach = min(-(-(base + sub_rows) // 128) * 128, seq)
        head_of = lax.broadcasted_iota(jnp.int32, (ATT_ROWS, local), 1)
        p_row = pos_row[m][:, :reach]

        @pl.loop(0, sub_rows // ATT_ROWS)
        def _(i):
            rows = pl.ds(pl.multiple_of(s * sub_rows + i * ATT_ROWS, ATT_ROWS), ATT_ROWS)
            first_row = base + i * ATT_ROWS
            p_col = pos_col[pl.ds(pl.multiple_of(m * seq + first_row, ATT_ROWS), ATT_ROWS), :]
            rel = p_col - p_row
            keep = (lax.broadcasted_iota(jnp.int32, (ATT_ROWS, reach), 0) + first_row) >= lax.broadcasted_iota(jnp.int32, (ATT_ROWS, reach), 1)
            q_all = q[rows, :]
            total = jnp.zeros((ATT_ROWS, local), F32)
            for h in range(n_local):
                mine = (head_of >= h * head_dim) & (head_of < (h + 1) * head_dim)
                q_h = jnp.where(mine, q_all, jnp.zeros_like(q_all))
                sc = lax.dot_general(q_h, kc[:reach, :], (((1,), (1,)), ((), ())), preferred_element_type=F32)
                sc = sc * (head_dim ** -0.5) - slopes[h] * rel
                sc = jnp.where(keep, sc, -1e30)
                top = jnp.max(sc, axis=-1, keepdims=True)
                e = jnp.exp(sc - top)
                p = (e * (1.0 / jnp.sum(e, axis=-1, keepdims=True))).astype(BF16)
                o = jnp.dot(p, vc[:reach, :], preferred_element_type=F32)
                total = jnp.where(mine, o, total)
            ctx[rows, pl.ds(pl.multiple_of(me * local, 128), local)] = total.astype(BF16)

    def attend_sub(m, c, s):
        for c_static in range(chunks):
            @pl.when(c == c_static)
            def _():
                attention(m, c_static, s)

    def step(unit, carry):
        m, c = unit // chunks, unit % chunks
        slot = lax.rem(unit, 2)
        h = hin.at[slot]

        @pl.when(first)
        def _():
            @pl.when(unit + 1 < units)
            def _():
                fetch(unit + 1, lax.rem(unit + 1, 2)).start()
            fetch(unit, slot).wait()

        @pl.when(jnp.logical_not(first))
        def _():
            pltpu.make_async_remote_copy(src_ref=hout, dst_ref=h, send_sem=psend.at[0], recv_sem=precv.at[slot],
                                         device_id={"pp": before}, device_id_type=MESH).wait_recv()

        norm_into(h, 0, size, ln_p[0:1, :], ln_p[1:2, :])
        here = pl.ds(pl.multiple_of(c * size, 64), size)
        for j, (dst, rows) in enumerate(((q, pl.ds(0, size)), (kc, here), (vc, here))):
            cols = slice(j * local, (j + 1) * local)
            dst[rows, :] = (jnp.dot(a[...], wq[:, cols], preferred_element_type=F32) + b_qkv[:, cols]).astype(BF16)

        @pl.when(unit > 0)
        def _():
            tail_one(unit - 1)
        for s in subs:
            attend_sub(m, c, s)
            gather_ctx[s].start()
            if s > 0:
                gather_ctx[s - 1].forward()
            if s == 0:
                @pl.when(unit > 0)
                def _():
                    tail_two(unit - 1)
        if SUBS == 1:
            gather_ctx[0].forward()

        @pl.when(unit > 0)
        def _():
            tail_three(unit - 1)

        @pl.when(first & (unit == 0))
        def _():
            gather_wo.forward()
            finish_wo()

        for s in subs:
            rows = pl.ds(s * sub_rows, sub_rows)
            gather_ctx[s].wait_near()
            gather_ctx[s].wait_far()

            @pl.loop(0, width // COLS)
            def _(j):
                cols = pl.ds(pl.multiple_of(j * COLS, COLS), COLS)
                y = jnp.dot(ctx[rows, :], wo[:, cols], preferred_element_type=F32)
                xmid[rows, cols] = (h[rows, cols].astype(F32) + y + b_res[0:1, cols]).astype(BF16)

            if s + 1 == SUBS:
                @pl.when(jnp.logical_not(first) & (unit < units - 2))
                def _():
                    pl.semaphore_signal(credit, inc=1, device_id={"pp": before}, device_id_type=MESH)
            norm_into(xmid, s * sub_rows, sub_rows, ln_p[2:3, :], ln_p[3:4, :])
            if s == SUBS - 2:
                gather_ctx[s + 1].forward()
            if s > 0:
                if s == 1:
                    @pl.when(unit > 0)
                    def _():
                        finish_out(unit - 1)
                reduce_middle(s - 1)

            @pl.loop(0, ff // COLS)
            def _(j):
                cols = pl.ds(pl.multiple_of(j * COLS, COLS), COLS)
                y = jnp.dot(a[rows, :], wu[:, cols], preferred_element_type=F32) + b_up[:, cols]
                u[rows, cols] = jax.nn.gelu(y, approximate=True).astype(BF16)

            if s > 0:
                reduce_end(s - 1, unit)

            @pl.loop(0, width // COLS)
            def _(j):
                cols = pl.ds(pl.multiple_of(j * COLS, COLS), COLS)
                part[rows, cols] = jnp.dot(u[rows, :], wd[:, cols], preferred_element_type=F32).astype(BF16)

            for copy in copies_first(s):
                copy.start()
        for s in subs:
            gather_ctx[s].wait_send()
        return carry

    lax.fori_loop(0, units, step, 0)
    tail_one(units - 1)
    tail_two(units - 1)
    tail_three(units - 1)
    finish_out(units - 1)


def solution(mesh):
    tp_size = mesh.shape["tp"]
    stages = mesh.shape["pp"]
    assert tp_size == 4

    def stage_body(hidden_in, positions, ln_params, w_qkv, b_qkv, w_out, w_up, b_up, w_down, b_res):
        n_micro, n_rows, seq, width = hidden_in.shape
        n_micro = n_micro * n_rows
        n_local, head_dim = w_qkv.shape[3], w_qkv.shape[4]
        local = n_local * head_dim
        ff = w_up.shape[2]
        size = seq // CHUNKS
        most = split_quarter(0, size // SUBS)[0][1]
        head_ids = (lax.axis_index("tp") * n_local + jnp.arange(n_local)).astype(F32)
        slopes = jnp.exp2(-8.0 * (head_ids + 1.0) / (n_local * tp_size))
        pos = positions.reshape(n_micro, seq).astype(F32)
        dims = (n_micro, seq, width, n_local, head_dim, CHUNKS, stages)
        hbm = pl.BlockSpec(memory_space=pl.ANY)
        vmem = pl.BlockSpec(memory_space=pltpu.VMEM)
        smem = pl.BlockSpec(memory_space=pltpu.SMEM)
        dma = pltpu.SemaphoreType.DMA
        acts = pl.pallas_call(
            functools.partial(pipeline_kernel, dims),
            out_shape=jax.ShapeDtypeStruct((n_micro, seq, width), BF16),
            in_specs=[smem, hbm, vmem, vmem, vmem, hbm, vmem, hbm, hbm, vmem, hbm, vmem],
            out_specs=hbm,
            scratch_shapes=[
                pltpu.VMEM((width, 3 * local), BF16), pltpu.VMEM((tp_size * local, width), BF16),
                pltpu.VMEM((width, ff), BF16), pltpu.VMEM((ff, width), BF16),
                pltpu.VMEM((2, size, width), BF16), pltpu.VMEM((size, width), BF16),
                pltpu.VMEM((size, local), BF16), pltpu.VMEM((seq, local), BF16), pltpu.VMEM((seq, local), BF16),
                pltpu.VMEM((size, tp_size * local), BF16), pltpu.VMEM((size, width), BF16),
                pltpu.VMEM((size, ff), BF16), pltpu.VMEM((size, width), BF16),
                pltpu.VMEM((SUBS, 2, most, width), BF16), pltpu.VMEM((SUBS, 2, 2, most, width), BF16), pltpu.VMEM((SUBS, 2, most, width), BF16),
                pltpu.VMEM((size, width), BF16),
                dma((4,)), dma((6 * SUBS,)), dma((6 * SUBS,)), dma((6 * SUBS,)), dma((6 * SUBS,)), dma((6 * SUBS,)), dma((6 * SUBS,)), dma((6,)), dma((6,)),
                dma((4 * SUBS,)), dma((2,)), dma((1,)), pltpu.SemaphoreType.REGULAR,
            ],
            compiler_params=pltpu.CompilerParams(collective_id=0, has_side_effects=True, vmem_limit_bytes=60 * 1024 * 1024),
        )(slopes, hidden_in.reshape(n_micro, seq, width), pos.reshape(n_micro * seq, 1), pos.reshape(n_micro, 1, seq), ln_params[0],
          w_qkv[0].reshape(width, 3 * local), b_qkv.reshape(1, 3 * local), w_out[0].reshape(local, width), w_up[0], b_up, w_down[0], b_res[0])
        return acts.reshape((1,) + hidden_in.shape)

    in_specs = (P(None, "dp", None, None), P(None, "dp", None), P("pp", None, None), P("pp", None, None, "tp", None), P("pp", None, "tp", None), P("pp", "tp", None, None), P("pp", None, "tp"), P("pp", "tp"), P("pp", "tp", None), P("pp", None, None))
    return jax.shard_map(stage_body, mesh=mesh, in_specs=in_specs, out_specs=P("pp", None, "dp", None, None), check_vma=False)
```

time: 2620 us -> 1010 us (0.39); the launches traced: 2590 us -> 1010 us
  waiting for transfers between devices: 1810 us -> 0 us
  Pallas kernels: 0 us -> 991 us
  matrix products: 442 us -> 0 us
  other arithmetic: 213 us -> 1.33 us
  local copies, waits for them, and re-layouts: 99.2 us -> 21.9 us
    psum x26 -> x0, waiting for transfers between devices: 1730 us -> none  [the longest x13 1030 us: stage_layer(): attn_sum = lax.psum(attn_part, 'tp')]
    pallas_call x0 -> x1, Pallas kernels: none -> 991 us  [stage_body(): pl.pallas_call(functools.partial(pipeline_kernel, dims), out_shape=jax.Sh...]
    dot_general x26 -> x0, matrix products: 275 us -> none  [the longest x13 176 us: stage_layer(): jnp.einsum('bsf,fd->bsd', gelu_out, w_down, preferred_element_type=jnp.fl...]
    sub x13 -> x0, matrix products: 126 us -> none  [attend(): probs_bf = jax.nn.softmax(scores, axis=-1).astype(jnp.bfloat16)]
    reduce_sum x52 -> x0, other arithmetic: 95.8 us -> none  [the longest x26 76.2 us: layer_norm(): row_mean = jnp.mean(hid_f32, axis=-1, keepdims=True)]
    dynamic_update_slice x13 -> x0, other arithmetic: 73.1 us -> none  [tick_step(): lax.dynamic_update_index_in_dim(stage_acts, jnp.where(is_valid, result, p...]
    ppermute x13 -> x0, waiting for transfers between devices: 72.4 us -> none  [tick_step(): sent_out = lax.ppermute(result, 'pp', perm=shift_perm)]
    dynamic_slice x26 -> x0, local copies, waits for them, and re-layouts: 53.5 us -> none  [the longest x13 44.4 us: tick_step(): lax.dynamic_index_in_dim(stage_acts, micro_idx, 0, keepdims=False)]
  transfers between devices with their start and end apart: 39 -> 0, of which waited for: 39 -> 0; matrix products, arithmetic and copies ran while one was open for 2% -> 0% of each run, Pallas kernels for 0% -> 0%
where the time goes in v1:
time: 1010 us
  Pallas kernels  991 us (98%)
  local copies, waits for them, and re-layouts  21.9 us (2%)
    pallas_call x1, Pallas kernels, stage_body(): pl.pallas_call(functools.partial(pipeline_kernel, dims), out_shape=jax.Sh...  991 us

profile of v1, /device:TPU:103, one launch (start us, length us, event | category | flops | bytes accessed | tf_op | source)
XLA Modules:
  0.0 1014.2 jit_solution(5080010190421696496)
XLA Ops:
  0.0 0.6 multiply_exponential_fusion.slopes
  0.6 1.4 reshape.24.b_qkv
  2.0 0.7 convert_element_type.18.pos_row
  2.7 0.0 copy-start
  2.7 2.1 copy.14.pos_col
  4.8 5.7 copy.15.w_qkv
  10.5 0.0 copy-done
  10.5 990.9 %shard_map.100 = bf16[6,768,1536]{2,1,0:T(8,128)(2,1)} custom-call(f32[4]{0:T(128)} %multiply_exponential_fusion.slopes, bf16[6,768,1536]{2,1,0:T(8,128)(2,1)} %bitcast.12, f32[4608,1]{1,0:T(8,128)} %copy.14.pos_col, f32[6,1,768]{2,1,0:T(1,128)} %copy-done, f32[4,1536]{1,0:T(4,128)} %bitcast.18, bf16[1536,1152]{1,0:T(8,128)(2,1)} %copy.15.w_qkv, ...), custom_call_target="tpu_custom_call" | custom-call | tf_op jit(solution)/shard_map/pallas_call | solution.py:407
  1001.5 12.7 %copy.18 = bf16[1,6,1,768,1536]{4,3,2,1,0:T(8,128)(2,1)} copy(bf16[1,6,1,768,1536]{4,3,2,1,0:T(8,128)(2,1)} %bitcast.11) | data formatting | bytes 28311552
Async XLA Ops:
  2.7 7.8 copy-start

commit v2 on v1

v2 whole, which is shorter than its diff:
```python
import functools

import jax
import jax.numpy as jnp
from jax import lax
from jax.experimental import pallas as pl
from jax.experimental.pallas import tpu as pltpu
from jax.sharding import PartitionSpec as P

MESH = pl.DeviceIdType.MESH
F32 = jnp.float32
BF16 = jnp.bfloat16
CHUNKS = 3
LN_ROWS = 32
HEAD_UNROLL = 4
COLS = 1536


class RingGather:
    def __init__(self, view, me, left, right, send, recv, base=0):
        self.view, self.me, self.left, self.right = view, me, left, right
        self.send, self.recv, self.base = send, recv, base

    def _copy(self, owner, half, slot, to):
        ref = self.view(owner, half)
        return pltpu.make_async_remote_copy(
            src_ref=ref, dst_ref=ref, send_sem=self.send.at[self.base + slot], recv_sem=self.recv.at[self.base + slot],
            device_id={"tp": to}, device_id_type=MESH)

    def start(self):
        self._copy(self.me, 0, 0, self.right).start()
        self._copy(self.me, 1, 3, self.left).start()
        self._copy(self.me, 1, 1, self.right).start()
        self._copy(self.me, 0, 4, self.left).start()

    def start_half(self, half):
        self._copy(self.me, half, half, self.right).start()
        self._copy(self.me, half, 4 - half, self.left).start()

    def forward(self):
        self._copy(self.left, 0, 0, self.right).wait_recv()
        self._copy(self.left, 0, 2, self.right).start()
        self._copy(self.right, 1, 3, self.left).wait_recv()
        self._copy(self.right, 1, 5, self.left).start()

    def wait_near(self):
        self._copy(self.left, 1, 1, self.right).wait_recv()
        self._copy(self.right, 0, 4, self.left).wait_recv()

    def wait_far(self):
        far = lax.rem(self.me + 2, 4)
        self._copy(far, 0, 2, self.right).wait_recv()
        self._copy(far, 1, 5, self.left).wait_recv()

    def wait_send(self):
        for slot, owner, half, to in ((0, self.me, 0, self.right), (1, self.me, 1, self.right), (2, self.left, 0, self.right),
                                      (3, self.me, 1, self.left), (4, self.me, 0, self.left), (5, self.right, 1, self.left)):
            self._copy(owner, half, slot, to).wait_send()


def norm_rows(x, gain, shift):
    mean = jnp.mean(x, axis=-1, keepdims=True)
    cent = x - mean
    var = jnp.mean(cent * cent, axis=-1, keepdims=True)
    return (cent * lax.rsqrt(var + 1e-5) * gain + shift).astype(BF16)


def pipeline_kernel(dims, slopes, hidden, pos_col, pos_row, ln_p, w_qkv, b_qkv, w_out, w_up, b_up, w_down, b_res, acts,
                    wq, wo, wu, wd, hin, a, qkv, ctx, xmid, u, part, r1, r2, msg, hout,
                    wsem, asend, arecv, rsend, rrecv, bsend, brecv, wsend, wrecv, psend, precv, osem, credit):
    n_micro, seq, width, n_local, head_dim, chunks, stages = dims
    size = seq // chunks
    quarter, half = size // 4, size // 8
    local = n_local * head_dim
    units = n_micro * chunks
    ff = wu.shape[1]
    me = lax.axis_index("tp")
    stage = lax.axis_index("pp")
    left, right, far = lax.rem(me + 3, 4), lax.rem(me + 1, 4), lax.rem(me + 2, 4)
    before, after = lax.rem(stage + stages - 1, stages), lax.rem(stage + 1, stages)
    first, last = stage == 0, stage == stages - 1
    inner = jnp.logical_not(last)

    def wo_rows(owner, part_id):
        return wo.at[pl.ds(pl.multiple_of(owner * local + part_id * (local // 2), 64), local // 2)]

    own_wo = wo.at[pl.ds(pl.multiple_of(me * local, 128), local)]
    loads = [pltpu.make_async_copy(w_out, own_wo, wsem.at[0]), pltpu.make_async_copy(w_qkv, wq, wsem.at[1]),
             pltpu.make_async_copy(w_up, wu, wsem.at[2]), pltpu.make_async_copy(w_down, wd, wsem.at[3])]
    for load in loads:
        load.start()

    def fetch(unit, slot):
        m, c = unit // chunks, unit % chunks
        return pltpu.make_async_copy(hidden.at[m, pl.ds(pl.multiple_of(c * size, 64), size)], hin.at[slot], precv.at[slot])

    @pl.when(first)
    def _():
        fetch(0, 0).start()

    barrier = pltpu.get_barrier_semaphore()
    for peer in (left, right):
        pl.semaphore_signal(barrier, inc=1, device_id={"tp": peer}, device_id_type=MESH)
    for peer in (before, after):
        pl.semaphore_signal(barrier, inc=1, device_id={"pp": peer}, device_id_type=MESH)
    qkv[...] = jnp.zeros_like(qkv)
    pl.semaphore_wait(barrier, 4)

    loads[0].wait()
    gather_wo = RingGather(wo_rows, me, left, right, wsend, wrecv)
    gather_wo.start()
    for load in loads[1:]:
        load.wait()

    def finish_wo():
        gather_wo.wait_near()
        gather_wo.wait_far()
        gather_wo.wait_send()

    @pl.when(jnp.logical_not(first))
    def _():
        gather_wo.forward()
        finish_wo()

    def part_rows(owner, k):
        return pl.ds(pl.multiple_of(owner * quarter + k * half, 8), half)

    def quarter_rows(owner):
        return pl.ds(pl.multiple_of(owner * quarter, 16), quarter)

    def gather_ctx(unit):
        parity = lax.rem(unit, 2)

        def view(owner, k):
            return ctx.at[parity, pl.ds(k * (size // 2), size // 2), pl.ds(pl.multiple_of(owner * local, 128), local)]
        return RingGather(view, me, left, right, asend, arecv, 6 * parity)

    def gather_out(unit):
        parity = lax.rem(unit, 2)
        return RingGather(lambda owner, k: hout.at[parity, part_rows(owner, k)], me, left, right, bsend, brecv)

    def reduce_copy(slot):
        src, dst, to = ((part.at[part_rows(far, 0)], r1.at[0], right), (part.at[part_rows(far, 1)], r1.at[1], left),
                        (part.at[part_rows(right, 1)], r2.at[0, 1], right), (part.at[part_rows(left, 0)], r2.at[1, 0], left),
                        (msg.at[0], r2.at[0, 0], right), (msg.at[1], r2.at[1, 1], left))[slot]
        return pltpu.make_async_remote_copy(src_ref=src, dst_ref=dst, send_sem=rsend.at[slot], recv_sem=rrecv.at[slot],
                                            device_id={"tp": to}, device_id_type=MESH)

    def hand_on(k, owner, unit):
        rows, slot = quarter_rows(owner), lax.rem(unit, 2)
        return pltpu.make_async_remote_copy(src_ref=hout.at[slot, rows], dst_ref=hin.at[slot, rows], send_sem=psend.at[4 * slot + k],
                                            recv_sem=precv.at[slot], device_id={"pp": after}, device_id_type=MESH)

    def reduce_middle():
        for k, owner in ((0, right), (1, left)):
            reduce_copy(k).wait_recv()
            msg[k] = (part[part_rows(owner, k), :].astype(F32) + r1[k].astype(F32)).astype(BF16)
            reduce_copy(4 + k).start()

    def reduce_end(unit):
        slot = lax.rem(unit, 2)
        for k in range(2, 6):
            reduce_copy(k).wait_recv()
        for k in range(2):
            rows = part_rows(me, k)
            y = part[rows, :].astype(F32) + r2[0, k].astype(F32) + r2[1, k].astype(F32)
            hout[slot, rows, :] = (xmid[rows, :].astype(F32) + y + b_res[1:2, :]).astype(BF16)
        gather_out(unit).start()

        @pl.when(inner & (unit > 1))
        def _():
            pl.semaphore_wait(credit, 1)

        @pl.when(inner)
        def _():
            hand_on(0, me, unit).start()
        for k in range(6):
            reduce_copy(k).wait_send()

    def out_near(unit):
        gather_out(unit).wait_near()

        @pl.when(inner)
        def _():
            hand_on(1, left, unit).start()
            hand_on(2, right, unit).start()

    def store_out(unit):
        m, c, slot = unit // chunks, unit % chunks, lax.rem(unit, 2)
        return pltpu.make_async_copy(hout.at[slot], acts.at[m, pl.ds(pl.multiple_of(c * size, 64), size)], osem.at[slot])

    def out_far(unit):
        gather_out(unit).wait_far()

        @pl.when(inner)
        def _():
            hand_on(3, far, unit).start()
        store_out(unit).start()
        gather_out(unit).wait_send()

    def finish_out(unit):
        store_out(unit).wait()

        @pl.when(inner)
        def _():
            for k, owner in enumerate((me, left, right, far)):
                hand_on(k, owner, unit).wait_send()

    def norm_into(src, start, count, gain, shift):
        @pl.loop(0, count // LN_ROWS)
        def _(i):
            rows = pl.ds(pl.multiple_of(start + i * LN_ROWS, LN_ROWS), LN_ROWS)
            a[rows, :] = norm_rows(src[rows, :].astype(F32), gain, shift)

    def attention(m, c_static, parity, gather):
        base, block = c_static * size, size // 2
        reach = min(-(-(base + size) // 128) * 128, seq)
        head_of = lax.broadcasted_iota(jnp.int32, (block, local), 1)
        p_row = pos_row[m][:, :reach]

        @pl.loop(0, 2)
        def _(i):
            first_row = base + i * block
            p_col = pos_col[pl.ds(pl.multiple_of(m * seq + first_row, 32), block), :]
            rel = p_col - p_row
            keep = (lax.broadcasted_iota(jnp.int32, (block, reach), 0) + first_row) >= lax.broadcasted_iota(jnp.int32, (block, reach), 1)
            q_all = qkv[0, pl.ds(pl.multiple_of(first_row, 32), block), :]

            def head(h, total):
                mine = (head_of >= h * head_dim) & (head_of < (h + 1) * head_dim)
                q_h = jnp.where(mine, q_all, jnp.zeros_like(q_all))
                sc = lax.dot_general(q_h, qkv[1, :reach, :], (((1,), (1,)), ((), ())), preferred_element_type=F32)
                sc = sc * (head_dim ** -0.5) - slopes[h] * rel
                sc = jnp.where(keep, sc, -1e30)
                top = jnp.max(sc, axis=-1, keepdims=True)
                e = jnp.exp(sc - top)
                p = (e * (1.0 / jnp.sum(e, axis=-1, keepdims=True))).astype(BF16)
                o = jnp.dot(p, qkv[2, :reach, :], preferred_element_type=F32)
                return jnp.where(mine, o, total)

            total = lax.fori_loop(0, n_local, head, jnp.zeros((block, local), F32), unroll=HEAD_UNROLL)
            ctx[parity, pl.ds(pl.multiple_of(i * block, 32), block), pl.ds(pl.multiple_of(me * local, 128), local)] = total.astype(BF16)
            gather.start_half(i)

    def step(unit, carry):
        m, c = unit // chunks, unit % chunks
        slot = lax.rem(unit, 2)
        h = hin.at[slot]
        ctx_now = gather_ctx(unit)

        @pl.when(first)
        def _():
            @pl.when(unit + 1 < units)
            def _():
                fetch(unit + 1, lax.rem(unit + 1, 2)).start()
            fetch(unit, slot).wait()

        @pl.when(jnp.logical_not(first))
        def _():
            pltpu.make_async_remote_copy(src_ref=hout.at[slot], dst_ref=h, send_sem=psend.at[0], recv_sem=precv.at[slot],
                                         device_id={"pp": before}, device_id_type=MESH).wait_recv()

        norm_into(h, 0, size, ln_p[0:1, :], ln_p[1:2, :])
        here = pl.ds(pl.multiple_of(c * size, 64), size)

        for j in range(3):
            cols = slice(j * local, (j + 1) * local)
            qkv[j, here, :] = (jnp.dot(a[...], wq[:, cols], preferred_element_type=F32) + b_qkv[:, cols]).astype(BF16)
        for c_static in range(chunks):
            @pl.when(c == c_static)
            def _():
                attention(m, c_static, slot, ctx_now)

        @pl.when(unit > 2)
        def _():
            finish_out(unit - 3)

        @pl.when(unit > 0)
        def _():
            reduce_middle()
        ctx_now.forward()

        @pl.when(unit > 0)
        def _():
            reduce_end(unit - 1)

        @pl.when(first & (unit == 0))
        def _():
            gather_wo.forward()
            finish_wo()
        ctx_now.wait_near()
        ctx_now.wait_far()

        @pl.loop(0, width // COLS)
        def _(j):
            cols = pl.ds(pl.multiple_of(j * COLS, COLS), COLS)
            y = jnp.dot(ctx[slot], wo[:, cols], preferred_element_type=F32)
            xmid[:, cols] = (h[:, cols].astype(F32) + y + b_res[0:1, cols]).astype(BF16)

        @pl.when(jnp.logical_not(first) & (unit < units - 2))
        def _():
            pl.semaphore_signal(credit, inc=1, device_id={"pp": before}, device_id_type=MESH)
        norm_into(xmid, 0, size, ln_p[2:3, :], ln_p[3:4, :])

        @pl.when(unit > 0)
        def _():
            gather_out(unit - 1).forward()

        @pl.loop(0, ff // COLS)
        def _(j):
            cols = pl.ds(pl.multiple_of(j * COLS, COLS), COLS)
            y = jnp.dot(a[...], wu[:, cols], preferred_element_type=F32) + b_up[:, cols]
            u[:, cols] = jax.nn.gelu(y, approximate=True).astype(BF16)

        @pl.when(unit > 0)
        def _():
            out_near(unit - 1)

        @pl.loop(0, width // COLS)
        def _(j):
            cols = pl.ds(pl.multiple_of(j * COLS, COLS), COLS)
            part[:, cols] = jnp.dot(u[...], wd[:, cols], preferred_element_type=F32).astype(BF16)

        ctx_now.wait_send()
        for k in range(4):
            reduce_copy(k).start()

        @pl.when(unit > 0)
        def _():
            out_far(unit - 1)
        return carry

    lax.fori_loop(0, units, step, 0)
    finish_out(units - 3)
    reduce_middle()
    reduce_end(units - 1)
    gather_out(units - 1).forward()
    out_near(units - 1)
    out_far(units - 1)
    finish_out(units - 2)
    finish_out(units - 1)


def solution(mesh):
    tp_size = mesh.shape["tp"]
    stages = mesh.shape["pp"]
    assert tp_size == 4

    def stage_body(hidden_in, positions, ln_params, w_qkv, b_qkv, w_out, w_up, b_up, w_down, b_res):
        n_micro, n_rows, seq, width = hidden_in.shape
        n_micro = n_micro * n_rows
        n_local, head_dim = w_qkv.shape[3], w_qkv.shape[4]
        local = n_local * head_dim
        ff = w_up.shape[2]
        size = seq // CHUNKS
        half = size // 8
        head_ids = (lax.axis_index("tp") * n_local + jnp.arange(n_local)).astype(F32)
        slopes = jnp.exp2(-8.0 * (head_ids + 1.0) / (n_local * tp_size))
        pos = positions.reshape(n_micro, seq).astype(F32)
        dims = (n_micro, seq, width, n_local, head_dim, CHUNKS, stages)
        hbm = pl.BlockSpec(memory_space=pl.ANY)
        vmem = pl.BlockSpec(memory_space=pltpu.VMEM)
        smem = pl.BlockSpec(memory_space=pltpu.SMEM)
        dma = pltpu.SemaphoreType.DMA
        acts = pl.pallas_call(
            functools.partial(pipeline_kernel, dims),
            out_shape=jax.ShapeDtypeStruct((n_micro, seq, width), BF16),
            in_specs=[smem, hbm, vmem, vmem, vmem, hbm, vmem, hbm, hbm, vmem, hbm, vmem],
            out_specs=hbm,
            scratch_shapes=[
                pltpu.VMEM((width, 3 * local), BF16), pltpu.VMEM((tp_size * local, width), BF16),
                pltpu.VMEM((width, ff), BF16), pltpu.VMEM((ff, width), BF16),
                pltpu.VMEM((2, size, width), BF16), pltpu.VMEM((size, width), BF16),
                pltpu.VMEM((3, seq, local), BF16),
                pltpu.VMEM((2, size, tp_size * local), BF16), pltpu.VMEM((size, width), BF16),
                pltpu.VMEM((size, ff), BF16), pltpu.VMEM((size, width), BF16),
                pltpu.VMEM((2, half, width), BF16), pltpu.VMEM((2, 2, half, width), BF16), pltpu.VMEM((2, half, width), BF16),
                pltpu.VMEM((2, size, width), BF16),
                dma((4,)), dma((12,)), dma((12,)), dma((6,)), dma((6,)), dma((6,)), dma((6,)), dma((6,)), dma((6,)),
                dma((8,)), dma((2,)), dma((2,)), pltpu.SemaphoreType.REGULAR,
            ],
            compiler_params=pltpu.CompilerParams(collective_id=0, has_side_effects=True, vmem_limit_bytes=60 * 1024 * 1024),
        )(slopes, hidden_in.reshape(n_micro, seq, width), pos.reshape(n_micro * seq, 1), pos.reshape(n_micro, 1, seq), ln_params[0],
          w_qkv[0].reshape(width, 3 * local), b_qkv.reshape(1, 3 * local), w_out[0].reshape(local, width), w_up[0], b_up, w_down[0], b_res[0])
        return acts.reshape((1,) + hidden_in.shape)

    in_specs = (P(None, "dp", None, None), P(None, "dp", None), P("pp", None, None), P("pp", None, None, "tp", None), P("pp", None, "tp", None), P("pp", "tp", None, None), P("pp", None, "tp"), P("pp", "tp"), P("pp", "tp", None), P("pp", None, None))
    return jax.shard_map(stage_body, mesh=mesh, in_specs=in_specs, out_specs=P("pp", None, "dp", None, None), check_vma=False)
```

time: 1010 us -> 863 us (0.85)
  Pallas kernels: 991 us -> 839 us
    pallas_call x1, Pallas kernels: 991 us -> 839 us  [stage_body(): pl.pallas_call(functools.partial(pipeline_kernel, dims), out_shape=jax.Sh...]
where the time goes in v2:
time: 863 us; the launch traced here: 862 us
  Pallas kernels  839 us (97%)
  local copies, waits for them, and re-layouts  21.9 us (3%)
    pallas_call x1, Pallas kernels, stage_body(): pl.pallas_call(functools.partial(pipeline_kernel, dims), out_shape=jax.Sh...  839 us

profile of v2, /device:TPU:103, one launch (start us, length us, event | category | flops | bytes accessed | tf_op | source)
XLA Modules:
  0.0 862.1 jit_solution(14232150128446600227)
XLA Ops:
  0.0 0.6 multiply_exponential_fusion.slopes
  0.6 1.4 reshape.24.b_qkv
  2.0 0.7 convert_element_type.18.pos_row
  2.7 0.0 copy-start
  2.7 2.1 copy.14.pos_col
  4.8 5.7 copy.15.w_qkv
  10.5 0.0 copy-done
  10.5 838.9 %shard_map.100 = bf16[6,768,1536]{2,1,0:T(8,128)(2,1)} custom-call(f32[4]{0:T(128)} %multiply_exponential_fusion.slopes, bf16[6,768,1536]{2,1,0:T(8,128)(2,1)} %bitcast.12, f32[4608,1]{1,0:T(8,128)} %copy.14.pos_col, f32[6,1,768]{2,1,0:T(1,128)} %copy-done, f32[4,1536]{1,0:T(4,128)} %bitcast.18, bf16[1536,1152]{1,0:T(8,128)(2,1)} %copy.15.w_qkv, ...), custom_call_target="tpu_custom_call" | custom-call | tf_op jit(solution)/shard_map/pallas_call | solution.py:365
  849.4 12.7 %copy.18 = bf16[1,6,1,768,1536]{4,3,2,1,0:T(8,128)(2,1)} copy(bf16[1,6,1,768,1536]{4,3,2,1,0:T(8,128)(2,1)} %bitcast.11) | data formatting | bytes 28311552
Async XLA Ops:
  2.7 7.8 copy-start
